TPU v7x, 256 devices: a whole 4x4x8 slice. The times are simulated.
256 devices in a mesh: tile: 64 (over z, y_hi, x), sub: 4 (over y_lo, core).
Axes of the slice: x: 4, y: 4 (y_hi: 2, y_lo: 2; y = y_hi * 2 + y_lo), z: 8, core: 2. Of those that a mesh axis runs over, the one named last changes fastest.
Arguments:
- grid_feats: bfloat16 [32768, 512], P(('tile', 'sub')), may hold values from -6 to 6
- mesh_feats: bfloat16 [32768, 512], P(('tile', 'sub')), may hold values from -6 to 6
- encode_edges: bfloat16 [262144, 512], P(('tile', 'sub')), may hold values from -6 to 6
- decode_edges: bfloat16 [131072, 512], P(('tile', 'sub')), may hold values from -6 to 6
- encode_source: int32 [262144], P(('tile', 'sub')), may hold values from 0 to 32767, as said below
- encode_target: int32 [262144], P(('tile', 'sub')), may hold values from -1 to 32767, as said below
- decode_source: int32 [131072], P(('tile', 'sub')), may hold values from 0 to 32767, as said below
- decode_target: int32 [131072], P(('tile', 'sub')), may hold values from -1 to 32767, as said below
- owner_fine: int32 [32768], P(('tile', 'sub')), may hold values from 0 to 8191, as said below
- owner_coarse: int32 [8192], P('tile'), may hold values from 0 to 511
- encode_weight: bfloat16 [512, 512], replicated, may hold values from -0.25 to 0.25
- decode_weight: bfloat16 [512, 512], replicated, may hold values from -0.25 to 0.25
- middle_weight: bfloat16 [512, 512], replicated, may hold values from -0.25 to 0.25
- summit_weight: bfloat16 [512, 512], replicated, may hold values from -0.25 to 0.25
- cotangent: bfloat16 [32768, 512], P(('tile', 'sub')), may hold values from -6 to 6
Outputs:
- grid_update: bfloat16 [32768, 512], P(('tile', 'sub'))
- encode_grad: float32 [512, 512], replicated
- decode_grad: float32 [512, 512], replicated
- middle_grad: float32 [512, 512], replicated
- summit_grad: float32 [512, 512], replicated
Inputs may be any that keep to these rules, and one draw needn't show every extreme that they name: `encode_source`: edge slot e is listed on device d = e // 1024; its source grid node lies on device d - 1, d or d + 1. `encode_target`: -1 marks padding; every other value is a mesh node of the device that lists the slot. On each device padding fills whole blocks of 128 slots after all live ones; every device has a live block, and some device has no padding. `decode_source`: edge slot e is listed on device d = e // 512; its source mesh node lies on device d - 1, d or d + 1. `decode_target`: -1 marks padding; every other value is a grid node of the device that lists the slot. On each device padding fills whole blocks of 128 slots after all live ones; every device has a live block, and some device has no padding. `owner_fine`: the middle node of fine mesh node m lies on the tile of the device that holds m.
All inputs are finite; a program needn't handle non-finite values.
Results may differ from a plain program's by a relative error of at most 0.012.
Values may be sent and summed in bfloat16 or wider, within the bound.
A program may use at most 64 MiB of HBM per device.

v0:
```python
import jax
import jax.numpy as jnp
from jax import lax
from jax.sharding import PartitionSpec as P

TOP_NODES = 512
BLOCK = 128


def with_halo(x, sides, width):
    edges = {}
    for axis, dim in sides:
        peers, length = (lax.axis_size(axis), x.shape[dim])
        up = [(i, (i + 1) % peers) for i in range(peers - 1)]
        last = lax.slice_in_dim(x, length - width, length, axis=dim)
        initial = lax.slice_in_dim(x, 0, width, axis=dim)
        edges[dim] = (
            lax.ppermute(last, axis, up),
            lax.ppermute(initial, axis, [(b, a) for a, b in up]),
        )
    done = []
    for _, dim in sides:
        low, high = edges[dim]
        around = [(width, width) if d in done else (0, 0) for d in range(x.ndim)]
        x = jnp.concatenate([jnp.pad(low, around), x, jnp.pad(high, around)], axis=dim)
        done.append(dim)
    return x


def copy_for_each(x, axis):
    peers = lax.axis_size(axis)
    return lax.all_to_all(jnp.broadcast_to(x[None], (peers, *x.shape)), axis, 0, 0, tiled=True)


def taken_together(x, axis):
    return copy_for_each(x, axis).sum(axis=0)


def split_up(x, dim, peers):
    dims = x.shape
    pieces = x.reshape(*dims[:dim], peers, dims[dim] // peers, *dims[dim + 1 :])
    return jnp.moveaxis(pieces, dim, 0)


def summed_on_arrival(x, axis, dim):
    pieces = split_up(x, dim, lax.axis_size(axis))
    arrived = lax.all_to_all(pieces, axis, split_axis=0, concat_axis=0, tiled=True)
    return arrived.sum(axis=0)


def joined_along(pieces, dim):
    dims = list(pieces.shape[1:])
    dims[dim] *= pieces.shape[0]
    return jnp.moveaxis(pieces, 0, dim).reshape(dims)


def gather_directly(x, axis, dim):
    return joined_along(copy_for_each(x, axis), dim)


def from_behind(x, axis, by):
    peers = lax.axis_size(axis)
    pairs = [(i, i + by) for i in range(peers) if 0 <= i + by < peers]
    return lax.ppermute(x, axis, pairs)


def silu_slope(values):
    sigmoid = jax.nn.sigmoid(values)
    return sigmoid * (1.0 + values * (1.0 - sigmoid))


def live_count(targets):
    heads = targets.reshape(-1, BLOCK)[:, 0]
    return jnp.sum((heads >= 0).astype(jnp.int32))


def local_targets(targets, first, limit):
    return jnp.where(targets >= 0, targets - first, limit)


def outer_sum(left, right):
    return lax.dot_general(
        left, right, (((0,), (0,)), ((), ())), preferred_element_type=jnp.float32
    )


def times_transposed(left, right):
    return lax.dot_general(
        left, right, (((1,), (1,)), ((), ())), preferred_element_type=jnp.float32
    )


def membership(indices, rows, dtype):
    return (jnp.arange(rows, dtype=jnp.int32)[:, None] == indices[None, :]).astype(dtype)


def exact_sum(members, values):
    return jnp.dot(
        members, values, precision=lax.Precision.HIGHEST, preferred_element_type=jnp.float32
    )


def edge_forward(sources, senders, targets, edge_feats, weight, segments, blocks):
    features = weight.shape[1]

    def block_step(block_id, carried):
        summed, stored = carried
        offset = block_id * BLOCK
        picked = lax.dynamic_slice_in_dim(senders, offset, BLOCK)
        receivers = lax.dynamic_slice_in_dim(targets, offset, BLOCK)
        edge_part = lax.dynamic_slice_in_dim(edge_feats, offset, BLOCK, 0)
        fetched = jnp.take(sources, picked, axis=0)
        preact = jnp.dot(fetched, weight, preferred_element_type=jnp.float32) + edge_part.astype(
            jnp.float32
        )
        summed = summed + exact_sum(
            membership(receivers, segments, jnp.float32), jax.nn.silu(preact)
        )
        stored = lax.dynamic_update_slice_in_dim(stored, preact, offset, 0)
        return (summed, stored)

    start_sum = jnp.zeros((segments, features), jnp.float32)
    start_store = jnp.zeros((senders.shape[0], features), jnp.float32)
    return lax.fori_loop(0, blocks, block_step, (start_sum, start_store))


def edge_backward(
    sources, senders, targets, stored, weight, upstream, factor, blocks, returned_rows
):
    features = weight.shape[1]

    def block_step(block_id, carried):
        gradient, returned = carried
        offset = block_id * BLOCK
        picked = lax.dynamic_slice_in_dim(senders, offset, BLOCK)
        receivers = lax.dynamic_slice_in_dim(targets, offset, BLOCK)
        preact = lax.dynamic_slice_in_dim(stored, offset, BLOCK, 0)
        fetched = jnp.take(sources, picked, axis=0)
        incoming = jnp.take(upstream, receivers, axis=0).astype(jnp.float32) * factor
        slope = (incoming * silu_slope(preact)).astype(jnp.bfloat16)
        gradient = gradient + outer_sum(fetched, slope)
        if returned_rows:
            passed = times_transposed(slope, weight)
            returned = returned + exact_sum(membership(picked, returned_rows, jnp.float32), passed)
        return (gradient, returned)

    start_grad = jnp.zeros((features, features), jnp.float32)
    start_back = jnp.zeros((max(returned_rows, 1), features), jnp.float32)
    return lax.fori_loop(0, blocks, block_step, (start_grad, start_back))


def shards(
    grid_feats,
    mesh_feats,
    encode_edges,
    decode_edges,
    encode_source,
    encode_target,
    decode_source,
    decode_target,
    owner_fine,
    owner_coarse,
    encode_weight,
    decode_weight,
    middle_weight,
    summit_weight,
    cotangent,
):
    grid_rows = grid_feats.shape[0]
    mesh_rows = mesh_feats.shape[0]
    level_rows = owner_coarse.shape[0]
    tiles = lax.axis_size("tile")
    subs = lax.axis_size("sub")
    device = lax.axis_index(("tile", "sub"))
    tile_id = lax.axis_index("tile")
    encode_factor = mesh_rows / encode_source.shape[0]
    decode_factor = grid_rows / decode_source.shape[0]
    middle_factor = level_rows / (mesh_rows * subs)
    summit_factor = TOP_NODES / (level_rows * tiles)
    grid_wide = with_halo(grid_feats, ((("tile", "sub"), 0),), grid_rows)
    encode_senders = encode_source - (device - 1) * grid_rows
    encode_targets = local_targets(encode_target, device * mesh_rows, mesh_rows)
    encode_blocks = live_count(encode_target)
    encode_summed, encode_stored = edge_forward(
        grid_wide,
        encode_senders,
        encode_targets,
        encode_edges,
        encode_weight,
        mesh_rows,
        encode_blocks,
    )
    mesh_mid = (mesh_feats.astype(jnp.float32) + encode_factor * encode_summed).astype(jnp.bfloat16)
    fine_local = owner_fine - tile_id * level_rows
    fine_members = membership(fine_local, level_rows, jnp.bfloat16)
    middle_part = jnp.dot(fine_members, mesh_mid, preferred_element_type=jnp.float32)
    middle_sum = taken_together(middle_part, "sub")
    middle_in = (middle_factor * middle_sum).astype(jnp.bfloat16)
    middle_act = jnp.dot(middle_in, middle_weight, preferred_element_type=jnp.float32)
    middle_out = (middle_in.astype(jnp.float32) + jax.nn.silu(middle_act)).astype(jnp.bfloat16)
    top_members = membership(owner_coarse, TOP_NODES, jnp.bfloat16)
    summit_part = jnp.dot(top_members, middle_out, preferred_element_type=jnp.float32)
    summit_share = summed_on_arrival(summit_part, "tile", 0)
    summit_in = (summit_factor * summit_share).astype(jnp.bfloat16)
    summit_act = jnp.dot(summit_in, summit_weight, preferred_element_type=jnp.float32)
    summit_out = gather_directly(jax.nn.silu(summit_act).astype(jnp.bfloat16), "tile", 0)
    coarse_of = jnp.take(owner_coarse, fine_local)
    lifted = jnp.take(middle_out, fine_local, axis=0).astype(jnp.float32) + jnp.take(
        summit_out, coarse_of, axis=0
    ).astype(jnp.float32)
    mesh_out = (mesh_mid.astype(jnp.float32) + lifted).astype(jnp.bfloat16)
    mesh_wide = with_halo(mesh_out, ((("tile", "sub"), 0),), mesh_rows)
    decode_senders = decode_source - (device - 1) * mesh_rows
    decode_targets = local_targets(decode_target, device * grid_rows, grid_rows)
    decode_blocks = live_count(decode_target)
    decode_summed, decode_stored = edge_forward(
        mesh_wide,
        decode_senders,
        decode_targets,
        decode_edges,
        decode_weight,
        grid_rows,
        decode_blocks,
    )
    grid_update = (grid_feats.astype(jnp.float32) + decode_factor * decode_summed).astype(
        jnp.bfloat16
    )
    decode_local, decode_returned = edge_backward(
        mesh_wide,
        decode_senders,
        decode_targets,
        decode_stored,
        decode_weight,
        cotangent,
        decode_factor,
        decode_blocks,
        3 * mesh_rows,
    )
    from_next = from_behind(decode_returned[:mesh_rows], ("tile", "sub"), -1)
    from_prev = from_behind(decode_returned[2 * mesh_rows :], ("tile", "sub"), 1)
    mesh_grad = decode_returned[mesh_rows : 2 * mesh_rows] + from_next + from_prev
    level_part = exact_sum(fine_members.astype(jnp.float32), mesh_grad)
    level_grad = taken_together(level_part, "sub")
    summit_grad_part = exact_sum(top_members.astype(jnp.float32), level_grad)
    summit_grad_share = summed_on_arrival(summit_grad_part, "tile", 0)
    summit_slope = (summit_grad_share * silu_slope(summit_act)).astype(jnp.bfloat16)
    summit_local = outer_sum(summit_in, summit_slope)
    summit_back = gather_directly(
        times_transposed(summit_slope, summit_weight).astype(jnp.bfloat16), "tile", 0
    )
    level_total = level_grad + summit_factor * jnp.take(summit_back, owner_coarse, axis=0).astype(
        jnp.float32
    )
    middle_slope = (level_total * silu_slope(middle_act)).astype(jnp.bfloat16)
    middle_local = outer_sum(middle_in, middle_slope)
    middle_back = level_total + times_transposed(middle_slope, middle_weight)
    mesh_total = mesh_grad + middle_factor * jnp.take(middle_back, fine_local, axis=0)
    encode_local, unused_rows = edge_backward(
        grid_wide,
        encode_senders,
        encode_targets,
        encode_stored,
        encode_weight,
        mesh_total,
        encode_factor,
        encode_blocks,
        0,
    )
    sub_share = 1.0 / subs
    encode_grad, decode_grad, middle_grad, summit_grad = lax.psum(
        (encode_local, decode_local, sub_share * middle_local, sub_share * summit_local),
        ("tile", "sub"),
    )
    return (grid_update, encode_grad, decode_grad, middle_grad, summit_grad)


def solution(mesh):
    placed = (
        P(("tile", "sub"), None),
        P(("tile", "sub"), None),
        P(("tile", "sub"), None),
        P(("tile", "sub"), None),
        P(("tile", "sub")),
        P(("tile", "sub")),
        P(("tile", "sub")),
        P(("tile", "sub")),
        P(("tile", "sub")),
        P("tile"),
        P(),
        P(),
        P(),
        P(),
        P(("tile", "sub"), None),
    )
    return jax.shard_map(
        shards,
        mesh=mesh,
        in_specs=placed,
        out_specs=(P(("tile", "sub"), None), P(), P(), P(), P()),
        check_vma=False,
    )
```

profile of v0, /device:TPU:1, one launch (start us, length us, event | category | flops | bytes accessed | tf_op | source)
XLA Modules:
  0.0 634.9 jit_solution(1157762285381149726)
XLA Ops:
  7.2 4.7 collective-permute-start
  11.9 1.9 collective-permute-start.1
  18.4 1.6 broadcast_in_dim.117
  20.1 32.4 %while.46 = (s32[]{:T(128)}, f32[128,512]{1,0:T(8,128)S(1)}, f32[1024,512]{1,0:T(8,128)}, s32[]{:T(128)}, s32[1024]{0:T(1024)S(1)}, /*index=5*/s32[1024]{0:T(102...) while((s32[]{:T(128)}, f32[128,512]{1,0:T(8,128)S(1)}, ...), condition=%wide.region_3.5_spmd, body=%wide.region_2.4_spmd.sunk | while | flops 168314624 | bytes 2367415 | solution.py:124
  21.7 1.9 constant_dynamic-update-slice_fusion.7
  25.7 1.9 constant_dynamic-update-slice_fusion.7
  29.7 1.9 constant_dynamic-update-slice_fusion.7
  33.6 1.9 constant_dynamic-update-slice_fusion.7
  37.6 1.9 constant_dynamic-update-slice_fusion.7
  41.6 1.9 constant_dynamic-update-slice_fusion.7
  45.6 1.9 constant_dynamic-update-slice_fusion.7
  49.5 1.9 constant_dynamic-update-slice_fusion.7
  52.9 15.0 %all_to_all.30 = f32[4,128,512]{2,1,0:T(8,128)S(1)} all-to-all(f32[4,128,512]{2,1,0:T(8,128)S(1)} %broadcast_in_dim.120), channel_id=1, replica_groups=mesh['tile'=64,'sub'=4] {'sub'}, dimensions={0} | all-to-all | bytes 2097152 | tf_op jit(solution)/shard_map/all_to_all | solution.py:32
  69.2 41.0 %all_to_all.31 = f32[64,8,512]{2,1,0:T(8,128)S(1)} all-to-all(f32[64,8,512]{2,1,0:T(8,128)S(1)} %convolution_bitcast_fusion), channel_id=1, replica_groups=mesh['tile'=64,'sub'=4] {'tile'}, dimensions={0} | all-to-all | bytes 2097152 | tf_op jit(solution)/shard_map/all_to_all | solution.py:47
  112.0 9.3 %all-to-all-start.2 = ((bf16[64,8,512]{2,1,0:T(8,128)(2,1)}), bf16[64,8,512]{2,1,0:T(8,128)(2,1)S(1)}, u32[]{:S(2)}, u32[]{:S(2)}) async-start(bf16[64,8,512]{2,1,0:T(8,128)(2,1)} %broadcast_in_dim.123), calls=%async_computation.2 | async-start | bytes 1048576 | tf_op jit(solution)/shard_map/all_to_all | solution.py:32
  123.4 12.4 %all-to-all-done.2 = bf16[64,8,512]{2,1,0:T(8,128)(2,1)S(1)} async-done(((bf16[64,8,512]{2,1,0:T(8,128)(2,1)}), bf16[64,8,512]{2,1,0:T(8,128)(2,1)S(1)}, u32[]{:S(2)}, u32[]{:S(2)}) %all-to-all-start.2) | async-done | bytes 524320 | tf_op jit(solution)/shard_map/all_to_all | solution.py:32
  136.8 7.5 %collective-permute-start.2 = (bf16[128,512]{1,0:T(8,128)(2,1)S(1)}, bf16[128,512]{1,0:T(8,128)(2,1)S(1)}, u32[]{:S(2)}, u32[]{:S(2)}) collective-permute-start(bf16[128,512]{1,0:T(8,128)(2,1)S(1)} %add_convert_fusion.1), channel_id=1, source_target_pairs={{0,1},{1,2},{2,3},{3,4},{4,5},{5,6},{6,7},{7,8},{8,9},{9,10},{10,1... | collective-permute-start | bytes 393224 | tf_op jit(solution)/shard_map/ppermute | solution.py:18
  144.4 1.9 collective-permute-start.3
  147.6 3.0 collective-permute-done.3
  151.6 25.7 %while.47 = (s32[]{:T(128)}, f32[128,512]{1,0:T(8,128)}, f32[512,512]{1,0:T(8,128)S(1)}, s32[]{:T(128)}, s32[512]{0:T(512)}, /*index=5*/s32[512]{0:T(512)}, bf16...) while((s32[]{:T(128)}, f32[128,512]{1,0:T(8,128)}, ...), condition=%wide.region_7.10_spmd, body=%wide.region_6.9_spmd.sunk | while | flops 168314624 | bytes 2367799 | solution.py:124
  155.8 2.0 convolution_add_fusion.14
  162.1 2.0 convolution_add_fusion.14
  168.3 2.0 convolution_add_fusion.14
  174.6 2.0 convolution_add_fusion.14
  178.5 29.3 %while.48 = (s32[]{:T(128)}, f32[512,512]{1,0:T(8,128)S(1)}, f32[384,512]{1,0:T(8,128)S(1)}, s32[]{:T(128)}, s32[512]{0:T(512)}, /*index=5*/bf16[384,512]{1,0:T(...) while((s32[]{:T(128)}, f32[512,512]{1,0:T(8,128)S(1)}, ...), condition=%wide.region_9.12_spmd, body=%wide.region_8.11_spmd.sunk | while | flops 438357888 | bytes 8272603 | solution.py:149
  182.2 1.5 convolution_add_fusion.15
  189.4 1.5 convolution_add_fusion.15
  196.6 1.5 convolution_add_fusion.15
  203.7 1.5 convolution_add_fusion.15
  207.9 1.9 collective-permute-start.4
  209.8 3.6 collective-permute-start.5
  213.4 2.1 collective-permute-done.4
  219.5 4.3 all-to-all-start.3
  223.7 12.5 %all-to-all-done.3 = f32[4,128,512]{2,1,0:T(8,128)} async-done(((f32[4,128,512]{2,1,0:T(8,128)}), f32[4,128,512]{2,1,0:T(8,128)}, u32[]{:S(2)}, u32[]{:S(2)}) %all-to-all-start.3) | async-done | bytes 1048608 | tf_op jit(solution)/shard_map/all_to_all | solution.py:32
  238.2 46.3 %all_to_all.32 = f32[64,8,512]{2,1,0:T(8,128)S(1)} all-to-all(f32[64,8,512]{2,1,0:T(8,128)S(1)} %fusion.42), channel_id=1, replica_groups=mesh['tile'=64,'sub'=4] {'tile'}, dimensions={0} | all-to-all | bytes 2097152 | tf_op jit(solution)/shard_map/all_to_all | solution.py:47
  286.8 9.3 %all-to-all-start.5 = ((bf16[64,8,512]{2,1,0:T(8,128)(2,1)}), bf16[64,8,512]{2,1,0:T(8,128)(2,1)S(1)}, u32[]{:S(2)}, u32[]{:S(2)}) async-start(bf16[64,8,512]{2,1,0:T(8,128)(2,1)} %broadcast_in_dim.127), calls=%async_computation.5 | async-start | bytes 1048576 | tf_op jit(solution)/shard_map/all_to_all | solution.py:32
  297.6 13.2 %all-to-all-done.5 = bf16[64,8,512]{2,1,0:T(8,128)(2,1)S(1)} async-done(((bf16[64,8,512]{2,1,0:T(8,128)(2,1)}), bf16[64,8,512]{2,1,0:T(8,128)(2,1)S(1)}, u32[]{:S(2)}, u32[]{:S(2)}) %all-to-all-start.5) | async-done | bytes 524320 | tf_op jit(solution)/shard_map/all_to_all | solution.py:32
  315.5 37.1 %while.49 = (s32[]{:T(128)}, f32[512,512]{1,0:T(8,128)S(1)}, s32[]{:T(128)}, s32[1024]{0:T(1024)}, bf16[384,512]{1,0:T(8,128)(2,1)S(1)}, /*index=5*/s32[1024]{0:...) while((s32[]{:T(128)}, f32[512,512]{1,0:T(8,128)S(1)}, ...), condition=%wide.region_13.16_spmd, body=%wide.region_12.15_spmd.sunk | while | flops 68161032 | bytes 3551915 | solution.py:149
  318.6 1.5 convolution_add_fusion.17
  323.1 1.5 convolution_add_fusion.17
  327.7 1.5 convolution_add_fusion.17
  332.3 1.5 convolution_add_fusion.17
  336.8 1.5 convolution_add_fusion.17
  341.4 1.5 convolution_add_fusion.17
  345.9 1.5 convolution_add_fusion.17
  350.5 1.5 convolution_add_fusion.17
  354.6 268.1 %all-reduce.3.cloned.1.call-done = (f32[512,512]{1,0:T(8,128)}, f32[512,512]{1,0:T(8,128)}, f32[512,512]{1,0:T(8,128)}, f32[512,512]{1,0:T(8,128)}) async-done(((f32[512,512]{1,0:T(8,128)}, f32[512,512]{1,0:T(8,128)}, f32[512,512]{1,0:T(8,128)}, f32[512,512]{1,0:T(8,128)}), (f32[512,512]{1,0:T(8,128)}, f32[512,512]{1,0:T(8,128)}, f32[512,512]{1,0:T(8,128)}, ...) | async-done | bytes 4194320 | tf_op jit(solution)/shard_map/psum | solution.py:270
  622.7 2.4 copy.69
  (265 shorter events, 98.0 us)
Async XLA Ops:
  7.2 60.8 %copy-start = (bf16[512,512]{1,0:T(8,128)(2,1)S(1)}, bf16[512,512]{1,0:T(8,128)(2,1)}, u32[]{:S(2)}) copy-start(bf16[512,512]{1,0:T(8,128)(2,1)} %param.39) | copy-start | bytes 1572868
  7.2 12.9 %copy-start.5 = (bf16[512,512]{1,0:T(8,128)(2,1)S(1)}, bf16[512,512]{1,0:T(8,128)(2,1)}, u32[]{:S(2)}) copy-start(bf16[512,512]{1,0:T(8,128)(2,1)} %param.37) | copy-start | bytes 1572868
  7.2 9.4 %collective-permute-start = (bf16[128,512]{1,0:T(8,128)(2,1)}, bf16[128,512]{1,0:T(8,128)(2,1)S(1)}, u32[]{:S(2)}, u32[]{:S(2)}) collective-permute-start(bf16[128,512]{1,0:T(8,128)(2,1)} %param.27), channel_id=1, source_target_pairs={{0,1},{1,2},{2,3},{3,4},{4,5},{5,6},{6,7},{7,8},{8,9},{9,10},{10,1... | collective-permute-start | bytes 393224 | tf_op jit(solution)/shard_map/ppermute | solution.py:18
  11.9 6.5 %collective-permute-start.1 = (bf16[128,512]{1,0:T(8,128)(2,1)}, bf16[128,512]{1,0:T(8,128)(2,1)S(1)}, u32[]{:S(2)}, u32[]{:S(2)}) collective-permute-start(bf16[128,512]{1,0:T(8,128)(2,1)} %param.27), channel_id=1, source_target_pairs={{1,0},{2,1},{3,2},{4,3},{5,4},{6,5},{7,6},{8,7},{9,8},{10,9},{11,1... | collective-permute-start | bytes 393224 | tf_op jit(solution)/shard_map/ppermute | solution.py:19
  15.2 107.3 %copy-start.28 = (s32[128]{0:T(128)}, s32[128]{0:T(128)S(1)}, u32[]{:S(2)}) copy-start(s32[128]{0:T(128)S(1)} %get-tuple-element.301) | copy-start | bytes 1540
  20.1 32.5 %copy-start.19 = (bf16[128,512]{1,0:T(8,128)(2,1)S(1)}, bf16[128,512]{1,0:T(8,128)(2,1)}, u32[]{:S(2)}) copy-start(bf16[128,512]{1,0:T(8,128)(2,1)} %param.28) | copy-start | bytes 393220
  52.5 15.4 %copy-start.25 = (s32[1024]{0:T(1024)}, s32[1024]{0:T(1024)S(1)}, u32[]{:S(2)}) copy-start(s32[1024]{0:T(1024)S(1)} %get-tuple-element.774) | copy-start | bytes 12292
  52.5 15.4 %copy-start.26 = (s32[1024]{0:T(1024)}, s32[1024]{0:T(1024)S(1)}, u32[]{:S(2)}) copy-start(s32[1024]{0:T(1024)S(1)} %get-tuple-element.775) | copy-start | bytes 12292
  52.9 16.1 %copy-start.1 = (s32[128]{0:T(128)S(1)}, s32[128]{0:T(128)}, u32[]{:S(2)}) copy-start(s32[128]{0:T(128)} %param.36) | copy-start | bytes 1540
  68.0 1.0 copy-start.20
  69.0 41.4 %copy-start.9 = (bf16[512,512]{1,0:T(8,128)(2,1)S(1)}, bf16[512,512]{1,0:T(8,128)(2,1)}, u32[]{:S(2)}) copy-start(bf16[512,512]{1,0:T(8,128)(2,1)} %param.40) | copy-start | bytes 1572868
  110.3 1.6 copy-start.22
  112.0 23.9 %all-to-all-start.2 = ((bf16[64,8,512]{2,1,0:T(8,128)(2,1)}), bf16[64,8,512]{2,1,0:T(8,128)(2,1)S(1)}, u32[]{:S(2)}, u32[]{:S(2)}) async-start(bf16[64,8,512]{2,1,0:T(8,128)(2,1)} %broadcast_in_dim.123), calls=%async_computation.2 | async-start | bytes 1048576 | tf_op jit(solution)/shard_map/all_to_all | solution.py:32
  121.2 25.0 %copy-start.27 = (s32[512]{0:T(512)S(1)}, s32[512]{0:T(512)}, u32[]{:S(2)}) copy-start(s32[512]{0:T(512)} %param.34) | copy-start | bytes 6148
  121.2 25.0 %copy-start.32 = (s32[512]{0:T(512)S(1)}, s32[512]{0:T(512)}, u32[]{:S(2)}) copy-start(s32[512]{0:T(512)} %param.33) | copy-start | bytes 6148
  121.3 29.4 %copy-start.29 = (s32[1024]{0:T(1024)}, s32[1024]{0:T(1024)S(1)}, u32[]{:S(2)}) copy-start(s32[1024]{0:T(1024)S(1)} %pad_clamp_fusion.8) | copy-start | bytes 12292
  122.5 25.1 %copy-start.30 = (pred[128]{0:T(512)(128)(4,1)}, pred[128]{0:T(512)(128)(4,1)S(1)}, u32[]{:S(2)}) copy-start(pred[128]{0:T(512)(128)(4,1)S(1)} %get-tuple-element.299) | copy-start | bytes 388
  123.4 28.1 %copy-start.6 = (bf16[512,512]{1,0:T(8,128)(2,1)S(1)}, bf16[512,512]{1,0:T(8,128)(2,1)}, u32[]{:S(2)}) copy-start(bf16[512,512]{1,0:T(8,128)(2,1)} %param.38) | copy-start | bytes 1572868
  136.8 10.8 %collective-permute-start.2 = (bf16[128,512]{1,0:T(8,128)(2,1)S(1)}, bf16[128,512]{1,0:T(8,128)(2,1)S(1)}, u32[]{:S(2)}, u32[]{:S(2)}) collective-permute-start(bf16[128,512]{1,0:T(8,128)(2,1)S(1)} %add_convert_fusion.1), channel_id=1, source_target_pairs={{0,1},{1,2},{2,3},{3,4},{4,5},{5,6},{6,7},{7,8},{8,9},{9,10},{10,1... | collective-permute-start | bytes 393224 | tf_op jit(solution)/shard_map/ppermute | solution.py:18
  144.4 6.3 collective-permute-start.3
  151.6 26.9 %copy-start.2 = (bf16[128,512]{1,0:T(8,128)(2,1)S(1)}, bf16[128,512]{1,0:T(8,128)(2,1)}, u32[]{:S(2)}) copy-start(bf16[128,512]{1,0:T(8,128)(2,1)} %param.41) | copy-start | bytes 393220
  177.3 1.0 copy-start.8
  182.2 1.5 copy-start.7
  189.4 1.5 copy-start.7
  196.6 1.5 copy-start.7
  203.7 1.5 copy-start.7
  207.8 11.6 %copy-start.3 = (f32[512,512]{1,0:T(8,128)}, f32[512,512]{1,0:T(8,128)S(1)}, u32[]{:S(2)}) copy-start(f32[512,512]{1,0:T(8,128)S(1)} %get-tuple-element.208) | copy-start | bytes 3145732
  207.9 7.7 %collective-permute-start.4 = (f32[128,512]{1,0:T(8,128)S(1)}, f32[128,512]{1,0:T(8,128)S(1)}, u32[]{:S(2)}, u32[]{:S(2)}) collective-permute-start(f32[128,512]{1,0:T(8,128)S(1)} %get-tuple-element.310), channel_id=1, source_target_pairs={{1,0},{2,1},{3,2},{4,3},{5,4},{6,5},{7,6},{8,7},{9,8},{10,9},{11,1... | collective-permute-start | bytes 786440 | tf_op jit(solution)/shard_map/ppermute | solution.py:64
  209.8 6.9 %collective-permute-start.5 = (f32[128,512]{1,0:T(8,128)S(1)}, f32[128,512]{1,0:T(8,128)S(1)}, u32[]{:S(2)}, u32[]{:S(2)}) collective-permute-start(f32[128,512]{1,0:T(8,128)S(1)} %get-tuple-element.311), channel_id=1, source_target_pairs={{0,1},{1,2},{2,3},{3,4},{4,5},{5,6},{6,7},{7,8},{8,9},{9,10},{10,1... | collective-permute-start | bytes 786440 | tf_op jit(solution)/shard_map/ppermute | solution.py:64
  215.6 3.9 copy-start.13
  216.7 0.7 copy-start.15
  219.5 16.8 %all-to-all-start.3 = ((f32[4,128,512]{2,1,0:T(8,128)}), f32[4,128,512]{2,1,0:T(8,128)}, u32[]{:S(2)}, u32[]{:S(2)}) async-start(f32[4,128,512]{2,1,0:T(8,128)} %broadcast_in_dim.126), calls=%async_computation.3 | async-start | bytes 2097152 | tf_op jit(solution)/shard_map/all_to_all | solution.py:32
  237.6 47.0 %copy-start.24 = (f32[8,512]{1,0:T(8,128)S(1)}, f32[8,512]{1,0:T(8,128)}, u32[]{:S(2)}) copy-start(f32[8,512]{1,0:T(8,128)} %get-tuple-element.315) | copy-start | bytes 49156
  284.5 11.8 %copy-start.23 = (f32[8,512]{1,0:T(8,128)S(1)}, f32[8,512]{1,0:T(8,128)}, u32[]{:S(2)}) copy-start(f32[8,512]{1,0:T(8,128)} %copy-done.22) | copy-start | bytes 49156
  284.6 27.0 %copy-start.21 = (f32[128,512]{1,0:T(8,128)S(1)}, f32[128,512]{1,0:T(8,128)}, u32[]{:S(2)}) copy-start(f32[128,512]{1,0:T(8,128)} %copy-done.20) | copy-start | bytes 786436
  284.6 27.0 %copy-start.33 = (f32[128,512]{1,0:T(8,128)S(1)}, f32[128,512]{1,0:T(8,128)}, u32[]{:S(2)}) copy-start(f32[128,512]{1,0:T(8,128)} %get-tuple-element.313) | copy-start | bytes 786436
  286.8 24.0 %all-to-all-start.5 = ((bf16[64,8,512]{2,1,0:T(8,128)(2,1)}), bf16[64,8,512]{2,1,0:T(8,128)(2,1)S(1)}, u32[]{:S(2)}, u32[]{:S(2)}) async-start(bf16[64,8,512]{2,1,0:T(8,128)(2,1)} %broadcast_in_dim.127), calls=%async_computation.5 | async-start | bytes 1048576 | tf_op jit(solution)/shard_map/all_to_all | solution.py:32
  296.2 326.6 %all-reduce.3.cloned.1.call-start = ((), (), s32[]{:S(2)}) async-start(), calls=%async_computation.6 | async-start | bytes 8388608 | tf_op jit(solution)/shard_map/psum | solution.py:270
  313.0 2.2 copy-start.14
  313.0 2.2 copy-start.16
  313.0 2.2 copy-start.31
  352.6 1.0 copy-start.4
  352.6 1.1 copy-start.17
  352.6 1.3 copy-start.18
  622.7 2.4 copy-start.12
  622.7 3.4 copy-start.11
  625.1 1.9 copy-start.10
Sparse Core Ops, SparseCore 0:
  353.7 268.9 all-reduce.2
where the time goes:
time: 637 us; the launch traced here: 635 us
  waiting for transfers between devices  313 us (49%)
  blocking collectives  102 us (16%)
  matrix products  65.9 us (10%)
  local copies, waits for them, and re-layouts  53.2 us (8%)
  starting transfers between devices  44.5 us (7%)
  other arithmetic  22.2 us (3%)
  loops' own time  18.8 us (3%)
  between operations  14.7 us (2%)
    psum x1, waiting for transfers between devices, shards(): lax.psum((encode_local, decode_local, sub_share * middle_local, sub_share...  268 us
    all_to_all x2, blocking collectives, summed_on_arrival(): lax.all_to_all(pieces, axis, split_axis=0, concat_axis=0, tiled=True)  87.3 us
    all_to_all x3, waiting for transfers between devices, copy_for_each(): lax.all_to_all(jnp.broadcast_to(x[None], (peers, *x.shape)), axis, 0, 0,...  38.1 us
    all_to_all x3, starting transfers between devices, copy_for_each(): lax.all_to_all(jnp.broadcast_to(x[None], (peers, *x.shape)), axis, 0, 0,...  22.9 us
    dot_general x14, matrix products, outer_sum(): lax.dot_general(left, right, (((0,), (0,)), ((), ())), preferred_element_...  20.8 us
    gather x24, local copies, waits for them, and re-layouts, block_step(): fetched = jnp.take(sources, picked, axis=0)  20.4 us
    dot_general x12, matrix products, block_step(): jnp.dot(fetched, weight, preferred_element_type=jnp.float32)  20 us
    and x24, other arithmetic, block_step(): fetched = jnp.take(sources, picked, axis=0)  15.3 us
  transfers between devices with their start and end apart: 10, of which 8 were waited for; matrix products, arithmetic and copies ran while one was open for 1% of the time, Pallas kernels for 0%

commit v1 on v0

v1 whole, which is shorter than its diff:
```python
import functools

import jax
import jax.numpy as jnp
from jax import lax
from jax.experimental import pallas as pl
from jax.experimental.pallas import tpu as pltpu
from jax.sharding import PartitionSpec as P

MESH = pl.DeviceIdType.MESH
TOP = 512
LANES = 128
LAYOUT = {64: (8, 2, 4), 4: (2, 1, 2)}
F32 = jnp.float32
BF16 = jnp.bfloat16


def nn(a, b):
    return lax.dot_general(a, b, (((1,), (0,)), ((), ())), preferred_element_type=F32)


def nt(a, b):
    return lax.dot_general(a, b, (((1,), (1,)), ((), ())), preferred_element_type=F32)


def tn(a, b):
    return lax.dot_general(a, b, (((0,), (0,)), ((), ())), preferred_element_type=F32)


def silu_pair(v):
    s = 0.5 * jnp.tanh(0.5 * v) + 0.5
    return v * s, s * (1.0 + v * (1.0 - s))


def ones_where(mask):
    return jnp.where(mask, 1.0, 0.0).astype(BF16)


def sum_halves(members, values):
    high = values.astype(BF16)
    low = (values - high.astype(F32)).astype(BF16)
    return nn(members, high) + nn(members, low)


def chunks(count, size, body):
    def step(i, carry):
        body(pl.ds(pl.multiple_of(i * size, size), size))
        return carry

    lax.fori_loop(0, count, step, 0)


class Spot:
    def __init__(self, tiles):
        self.nz, self.nyh, self.nx = LAYOUT[tiles]
        self.ny = 2 * self.nyh
        self.plane = self.ny * self.nx
        tile, sub = lax.axis_index("tile"), lax.axis_index("sub")
        self.tile, self.sub = tile, sub
        self.x = lax.rem(tile, self.nx)
        self.z = lax.div(tile, self.nx * self.nyh)
        yh = lax.rem(lax.div(tile, self.nx), self.nyh)
        self.core = lax.rem(sub, 2)
        self.y = yh * 2 + lax.div(sub, 2)
        self.p = self.y * self.nx + self.x
        self.device = tile * 4 + sub
        self.tiles = tiles

    def at(self, z, y, x, core):
        return (
            (z * self.nyh + lax.div(y, 2)) * self.nx + x,
            lax.rem(y, 2) * 2 + core,
        )

    def partner(self):
        return (self.tile, self.sub + 1 - 2 * self.core)

    def across(self):
        return (self.tile, lax.rem(self.sub + 2, 4))

    def beside(self, by):
        d = lax.rem(self.device + by + 4 * self.tiles, 4 * self.tiles)
        return (lax.div(d, 4), lax.rem(d, 4))

    def in_plane(self, k):
        y = lax.rem(self.y + k // self.nx, self.ny)
        x = lax.rem(self.x + k % self.nx, self.nx)
        return y * self.nx + x, self.at(self.z, y, x, self.core)

    def in_column(self, j):
        return self.at(lax.rem(self.z + j, self.nz), self.y, self.x, self.core)


def remote(src, dst, send, recv, where):
    return pltpu.make_async_remote_copy(
        src_ref=src,
        dst_ref=dst,
        send_sem=send,
        recv_sem=recv,
        device_id=where,
        device_id_type=MESH,
    )


class Total:
    def __init__(self, spot, slot, bufs):
        self.spot, self.slot = spot, slot
        own, pair, half, planes, column, full, self.ps, self.pr, self.qs, self.qr, self.zs, self.zr = bufs
        self.own, self.pair, self.half = own.at[slot], pair.at[slot], half.at[slot]
        self.planes, self.column, self.full = planes.at[slot], column.at[slot], full.at[slot]
        self.rows = TOP // 2
        self.block = self.rows // spot.plane

    def half_of(self, core):
        return pl.ds(pl.multiple_of(core * self.rows, self.rows), self.rows)

    def my_rows(self):
        s = self.spot
        start = s.core * self.rows + s.p * self.block
        return pl.ds(pl.multiple_of(start, self.block), self.block)

    def pair_copy(self, n):
        s = self.spot
        if n == 0:
            src, dst = self.own.at[self.half_of(1 - s.core)], self.pair
        else:
            src = dst = self.full.at[self.half_of(s.core)]
        return remote(src, dst, self.ps.at[self.slot, n], self.pr.at[self.slot, n], s.partner())

    def plane_copy(self, n, k):
        q, where = self.spot.in_plane(k)
        if n == 0:
            src = self.half.at[pl.ds(pl.multiple_of(q * self.block, self.block), self.block)]
            dst = self.planes.at[k]
        else:
            src = dst = self.full.at[self.my_rows()]
        return remote(src, dst, self.qs.at[self.slot, n, k], self.qr.at[self.slot, n, k], where)

    def column_copy(self, j):
        s = self.spot
        src = self.column.at[s.z]
        return remote(src, src, self.zs.at[self.slot, j], self.zr.at[self.slot, j], s.in_column(j))

    def step0(self):
        self.pair_copy(0).start()

    def step1(self):
        self.pair_copy(0).wait_recv()
        mine = self.own[self.half_of(self.spot.core), :].astype(F32)
        self.half[...] = (mine + self.pair[...].astype(F32)).astype(BF16)
        for k in range(1, self.spot.plane):
            self.plane_copy(0, k).start()

    def step2(self):
        s = self.spot
        start = pl.multiple_of(s.p * self.block, self.block)
        total = self.half[pl.ds(start, self.block), :].astype(F32)
        for k in range(1, s.plane):
            self.plane_copy(0, k).wait_recv()
        for k in range(1, s.plane):
            total = total + self.planes[k].astype(F32)
        self.column[s.z] = total.astype(BF16)
        for j in range(1, s.nz):
            self.column_copy(j).start()

    def step3(self, scale=None):
        s = self.spot
        for j in range(1, s.nz):
            self.column_copy(j).wait_recv()
        total = self.column[0].astype(F32)
        for j in range(1, s.nz):
            total = total + self.column[j].astype(F32)
        if scale is not None:
            total = total * scale
        self.full[self.my_rows(), :] = total.astype(BF16)
        for k in range(1, s.plane):
            self.plane_copy(1, k).start()

    def step4(self):
        for k in range(1, self.spot.plane):
            self.plane_copy(1, k).wait_recv()
        self.pair_copy(1).start()

    def step5(self):
        self.pair_copy(1).wait_recv()

    def drain(self):
        for n in range(2):
            self.pair_copy(n).wait_send()
            for k in range(1, self.spot.plane):
                self.plane_copy(n, k).wait_send()
        for j in range(1, self.spot.nz):
            self.column_copy(j).wait_send()


def kernel(
    tiles,
    grid_hbm,
    mesh_hbm,
    ee_hbm,
    de_hbm,
    esrc,
    etgt,
    dsrc,
    dtgt,
    fine,
    coarse,
    we_hbm,
    wd_hbm,
    wm_hbm,
    ws_hbm,
    cot_hbm,
    out_grid,
    out_e,
    out_d,
    out_m,
    out_s,
    gw,
    mesh,
    ee,
    de,
    cot,
    we,
    wd,
    wm,
    ws,
    ids,
    se,
    ste,
    me,
    mte,
    sd,
    std,
    md,
    mtd,
    fm,
    ft,
    kt,
    kc,
    cw,
    cwt,
    sile,
    ssle,
    sild,
    ssld,
    mid,
    sub_src,
    sub_dst,
    midin,
    midss,
    midout,
    base,
    sumss,
    sumout,
    mow,
    slope,
    tw,
    rw,
    rback,
    lev,
    meshg,
    up,
    sslope,
    sback,
    own,
    pair,
    half,
    planes,
    column,
    full,
    lsem,
    hs,
    hr,
    ss,
    sr,
    ps,
    pr,
    qs,
    qr,
    zs,
    zr,
):
    n = LANES
    d = mesh.shape[1]
    spot = Spot(tiles)
    n_enc, n_dec = ee.shape[0], de.shape[0]
    enc_factor, dec_factor = n / n_enc, n / n_dec
    mid_factor, top_factor = 0.25, TOP / (n * tiles)
    bufs = (own, pair, half, planes, column, full, ps, pr, qs, qr, zs, zr)
    t_sum, t_back, t_dec, t_mid, t_enc = (Total(spot, i, bufs) for i in range(5))

    loads = [
        pltpu.make_async_copy(src, dst, lsem.at[i])
        for i, (src, dst) in enumerate(
            (
                (grid_hbm, gw.at[pl.ds(n, n)]),
                (we_hbm, we),
                (ee_hbm, ee),
                (mesh_hbm, mesh),
                (wm_hbm, wm),
                (ws_hbm, ws),
                (wd_hbm, wd),
                (de_hbm, de),
                (cot_hbm, cot),
            )
        )
    ]
    for copy in loads:
        copy.start()

    barrier = pltpu.get_barrier_semaphore()
    greeted = [spot.beside(1), spot.beside(-1), spot.partner(), spot.across()]
    greeted += [spot.in_plane(k)[1] for k in range(1, spot.plane)]
    greeted += [spot.in_column(j) for j in range(1, spot.nz)]
    for where in greeted:
        pl.semaphore_signal(barrier, inc=1, device_id=where, device_id_type=MESH)

    lane = lax.broadcasted_iota(jnp.int32, (n, n), 1)
    row = lax.broadcasted_iota(jnp.int32, (n, n), 0)

    def spread(ref, i, shift):
        across = jnp.broadcast_to(ref[i : i + 1, :] - shift, (n, n))
        return across, jnp.transpose(across)

    def fill(ref, i, shift, wide, by_edge, by_node):
        across, down = spread(ref, i, shift)
        for j in range(wide):
            by_edge[i * n : (i + 1) * n, j * n : (j + 1) * n] = ones_where(down == lane + j * n)
            by_node[j * n : (j + 1) * n, i * n : (i + 1) * n] = ones_where(across == row + j * n)

    first = spot.device * n
    across, down = spread(fine, 0, spot.tile * n)
    fm[...] = ones_where(across == row)
    ft[...] = ones_where(down == lane)
    across_c, down_c = spread(coarse, 0, 0)
    coarse_of = jnp.sum(jnp.where(across == row, down_c, 0).astype(F32), axis=0, keepdims=True)
    ids[1] = jnp.broadcast_to(coarse_of, (8, n))
    for i in range(n_enc // n):
        fill(esrc, i, first - n, 3, se, ste)
        fill(etgt, i, first, 1, mte, me)

    def beside_copy(src, dst, i, by):
        return remote(src, dst, hs.at[i], hr.at[i], spot.beside(by))

    def both_ways(ref, i, low, mid_at, high):
        return (
            beside_copy(ref.at[mid_at], ref.at[low], i, 1),
            beside_copy(ref.at[mid_at], ref.at[high], i + 1, -1),
        )

    low, middle, high = (pl.ds(i * n, n) for i in range(3))
    loads[0].wait()
    pl.semaphore_wait(barrier, len(greeted))
    grid_halo = both_ways(gw, 0, low, middle, high)
    ids_halo = both_ways(ids, 2, 0, 1, 2)
    for copy in grid_halo + ids_halo:
        copy.start()

    for i in range(n_dec // n):
        fill(dsrc, i, first - n, 3, sd, std)
        fill(dtgt, i, first, 1, mtd, md)
    for j in range(TOP // n):
        kt[:, j * n : (j + 1) * n] = ones_where(down_c == lane + j * n)
        kc[j * n : (j + 1) * n, :] = ones_where(across_c == row + j * n)

    loads[1].wait()
    loads[2].wait()
    for copy in grid_halo:
        copy.wait_recv()

    def encode(at):
        rows = nn(se[at, :], gw[...]).astype(BF16)
        act, sloped = silu_pair(nn(rows, we[...]) + ee[at, :].astype(F32))
        sile[at, :] = act.astype(BF16)
        ssle[at, :] = sloped

    chunks(n_enc // 256, 256, encode)
    loads[3].wait()
    mid_value = (mesh[...].astype(F32) + enc_factor * nn(me[...], sile[...])).astype(BF16)
    mid[...] = mid_value

    def sub_copy(i):
        where = spot.partner() if i % 2 == 0 else spot.across()
        return remote(sub_src.at[i], sub_dst.at[i], ss.at[i], sr.at[i], where)

    sub_src[0] = nn(fm[...], mid_value).astype(BF16)
    sub_copy(0).start()
    sub_copy(0).wait_recv()
    sub_src[1] = (sub_src[0].astype(F32) + sub_dst[0].astype(F32)).astype(BF16)
    sub_copy(1).start()
    loads[4].wait()
    sub_copy(1).wait_recv()
    middle_in = (mid_factor * (sub_src[1].astype(F32) + sub_dst[1].astype(F32))).astype(BF16)
    midin[...] = middle_in
    act, sloped = silu_pair(nn(middle_in, wm[...]))
    midss[...] = sloped
    middle_out = (middle_in.astype(F32) + act).astype(BF16)
    wide_row = lax.broadcasted_iota(jnp.int32, (n, d), 0)
    mine = (wide_row >= spot.sub * (n // 4)) & (wide_row < (spot.sub + 1) * (n // 4))
    midout[...] = jnp.where(mine, middle_out.astype(F32), 0.0).astype(BF16)
    t_sum.own[...] = nn(kc[...], midout[...]).astype(BF16)
    t_sum.step0()
    base[middle, :] = mid[...].astype(F32) + nn(ft[...], middle_out)
    t_sum.step1()
    base_halo = both_ways(base, 4, low, middle, high)
    for copy in base_halo:
        copy.start()
    for copy in ids_halo:
        copy.wait_recv()
    for i in range(3):
        around = jnp.broadcast_to(ids[i, 0:1, :].astype(jnp.int32), (n, n))
        along = jnp.transpose(around)
        for j in range(TOP // n):
            cw[j * n : (j + 1) * n, i * n : (i + 1) * n] = ones_where(around == row + j * n)
            cwt[i * n : (i + 1) * n, j * n : (j + 1) * n] = ones_where(along == lane + j * n)
    t_sum.step2()
    t_sum.step3(top_factor)
    for i in range(5, 9):
        loads[i].wait()
    for copy in base_halo:
        copy.wait_recv()
    t_sum.step4()
    t_sum.step5()

    def top(at):
        act, sloped = silu_pair(nn(t_sum.full[at, :], ws[...]))
        sumout[at, :] = act.astype(BF16)
        sumss[at, :] = sloped

    chunks(TOP // 256, 256, top)

    def lift(at):
        mow[at, :] = (base[at, :] + nn(cwt[at, :], sumout[...])).astype(BF16)

    chunks(3, n, lift)

    def decode(at):
        rows = nn(sd[at, :], mow[...]).astype(BF16)
        act, sloped = silu_pair(nn(rows, wd[...]) + de[at, :].astype(F32))
        sild[at, :] = act.astype(BF16)
        incoming = nn(mtd[at, :], cot[...]) * dec_factor
        slope[at, :] = (incoming * sloped).astype(BF16)

    chunks(n_dec // 256, 256, decode)

    def back(at):
        spread_slope = nn(std[at, :], slope[pl.ds(0, n_dec), :]).astype(BF16)
        tw[at, :] = spread_slope
        rw[at, :] = nt(spread_slope, wd[...]).astype(BF16)

    chunks(3, n, back)

    def top_part(at):
        t_back.own[at, :] = nn(cw[at, :], rw[...]).astype(BF16)

    chunks(TOP // 256, 256, top_part)
    t_back.step0()
    back_halo = (
        beside_copy(rw.at[high], rback.at[0], 6, 1),
        beside_copy(rw.at[low], rback.at[1], 7, -1),
    )
    t_back.step1()
    for copy in back_halo:
        copy.start()
    t_dec.own[...] = tn(mow[...], tw[...]).astype(BF16)
    t_dec.step0()
    out_grid[...] = (
        gw[middle, :].astype(F32) + dec_factor * nn(md[...], sild[...])
    ).astype(BF16)
    for copy in back_halo:
        copy.wait_recv()
    mesh_grad = rw[middle, :].astype(F32) + rback[0].astype(F32) + rback[1].astype(F32)
    meshg[...] = mesh_grad
    sub_src[2] = sum_halves(fm[...], mesh_grad).astype(BF16)
    sub_copy(2).start()
    t_back.step2()
    t_dec.step1()
    sub_copy(2).wait_recv()
    sub_src[3] = (sub_src[2].astype(F32) + sub_dst[2].astype(F32)).astype(BF16)
    sub_copy(3).start()
    t_back.step3()
    t_dec.step2()
    sub_copy(3).wait_recv()
    lev[...] = sub_src[3].astype(F32) + sub_dst[3].astype(F32)
    t_back.step4()
    t_back.step5()

    def top_slope(at):
        value = (t_back.full[at, :].astype(F32) * sumss[at, :]).astype(BF16)
        sslope[at, :] = value
        sback[at, :] = nt(value, ws[...]).astype(BF16)

    chunks(TOP // 256, 256, top_slope)
    level_total = lev[...] + top_factor * nn(kt[...], sback[...])
    middle_slope = (level_total * midss[...]).astype(BF16)
    own_slope = jnp.where(mine, middle_slope.astype(F32), 0.0).astype(BF16)
    t_mid.own[...] = tn(midin[...], own_slope).astype(BF16)
    t_mid.step0()
    middle_back = level_total + nt(middle_slope, wm[...])
    mesh_total = meshg[...] + mid_factor * nn(ft[...], middle_back.astype(BF16))
    up[...] = mesh_total.astype(BF16)

    def encode_back(at):
        upstream = nn(mte[at, :], up[...]) * enc_factor
        slope[at, :] = (upstream * ssle[at, :]).astype(BF16)

    chunks(n_enc // 256, 256, encode_back)

    def encode_spread(at):
        tw[at, :] = nn(ste[at, :], slope[...]).astype(BF16)

    chunks(3, n, encode_spread)
    t_enc.own[...] = tn(gw[...], tw[...]).astype(BF16)
    t_enc.step0()
    t_mid.step1()
    t_enc.step1()
    t_dec.step3()
    t_mid.step2()
    t_enc.step2()
    out_s[...] = tn(t_sum.full[...], sslope[...]).astype(BF16)
    t_mid.step3()
    t_enc.step3()
    t_dec.step4()
    t_mid.step4()
    t_enc.step4()
    for total, out in ((t_dec, out_d), (t_mid, out_m), (t_enc, out_e)):
        total.step5()
        out[...] = total.full[...]
    for total in (t_sum, t_back, t_dec, t_mid, t_enc):
        total.drain()
    for copy in grid_halo + ids_halo + base_halo + back_halo:
        copy.wait_send()
    for i in range(4):
        sub_copy(i).wait_send()


def shards(tiles, *args):
    (gf, mf, ee, de, es, et, ds, dt, fine, coarse, we, wd, wm, ws, cot) = args
    n, d = mf.shape
    ne, nd = ee.shape[0], de.shape[0]
    nz, nyh, nx = LAYOUT[tiles]
    plane = 2 * nyh * nx
    hbm = pl.BlockSpec(memory_space=pl.ANY)
    vmem = pl.BlockSpec(memory_space=pltpu.VMEM)

    def v(*shape, dtype=BF16):
        return pltpu.VMEM(shape, dtype)

    sem = lambda *shape: pltpu.SemaphoreType.DMA(shape)
    wide = 3 * n
    scratch = [
        v(wide, d),
        v(n, d),
        v(ne, d),
        v(nd, d),
        v(n, d),
        v(d, d),
        v(d, d),
        v(d, d),
        v(d, d),
        v(3, 8, n, dtype=F32),
        v(ne, wide),
        v(wide, ne),
        v(n, ne),
        v(ne, n),
        v(nd, wide),
        v(wide, nd),
        v(n, nd),
        v(nd, n),
        v(n, n),
        v(n, n),
        v(n, TOP),
        v(TOP, n),
        v(TOP, wide),
        v(wide, TOP),
        v(ne, d),
        v(ne, d, dtype=F32),
        v(nd, d),
        v(nd, d, dtype=F32),
        v(n, d),
        v(4, n, d),
        v(4, n, d),
        v(n, d),
        v(n, d, dtype=F32),
        v(n, d),
        v(wide, d, dtype=F32),
        v(TOP, d, dtype=F32),
        v(TOP, d),
        v(wide, d),
        v(ne, d),
        v(wide, d),
        v(wide, d),
        v(2, n, d),
        v(n, d, dtype=F32),
        v(n, d, dtype=F32),
        v(n, d),
        v(TOP, d),
        v(TOP, d),
        v(5, TOP, d),
        v(5, TOP // 2, d),
        v(5, TOP // 2, d),
        v(5, plane, TOP // 2 // plane, d),
        v(5, nz, TOP // 2 // plane, d),
        v(5, TOP, d),
        sem(9),
        sem(8),
        sem(8),
        sem(4),
        sem(4),
        sem(5, 2),
        sem(5, 2),
        sem(5, 2, plane),
        sem(5, 2, plane),
        sem(5, nz),
        sem(5, nz),
    ]
    grid_update, eg, dg, mg, sg = pl.pallas_call(
        functools.partial(kernel, tiles),
        out_shape=[jax.ShapeDtypeStruct((n, d), BF16)]
        + [jax.ShapeDtypeStruct((d, d), BF16)] * 4,
        in_specs=[hbm] * 4 + [vmem] * 6 + [hbm] * 5,
        out_specs=[vmem] * 5,
        scratch_shapes=scratch,
        compiler_params=pltpu.CompilerParams(
            collective_id=0, has_side_effects=True, vmem_limit_bytes=60 * 1024 * 1024
        ),
    )(
        gf,
        mf,
        ee,
        de,
        *(i.reshape(-1, LANES) for i in (es, et, ds, dt, fine, coarse)),
        we,
        wd,
        wm,
        ws,
        cot,
    )
    return (grid_update, *(g.astype(F32) for g in (eg, dg, mg, sg)))


def solution(mesh):
    rows, ids = P(("tile", "sub"), None), P(("tile", "sub"))
    placed = (rows,) * 4 + (ids,) * 5 + (P("tile"),) + (P(),) * 4 + (rows,)
    return jax.shard_map(
        functools.partial(shards, mesh.shape["tile"]),
        mesh=mesh,
        in_specs=placed,
        out_specs=(rows, P(), P(), P(), P()),
        check_vma=False,
    )
```

time: 637 us -> 116 us (0.18)
  waiting for transfers between devices: 313 us -> 0 us
  Pallas kernels: 0 us -> 109 us
  blocking collectives: 102 us -> 0 us
  matrix products: 65.9 us -> 0 us
  local copies, waits for them, and re-layouts: 53.2 us -> 0.67 us
  starting transfers between devices: 44.5 us -> 0 us
  loops' own time: 18.8 us -> 0 us
  other arithmetic: 22.2 us -> 5.5 us
  between operations: 14.7 us -> 0.66 us
    psum x1 -> x0, waiting for transfers between devices: 268 us -> none  [shards(): lax.psum((encode_local, decode_local, sub_share * middle_local, sub_share...]
    pallas_call x0 -> x1, Pallas kernels: none -> 109 us  [shards(): pl.pallas_call(functools.partial(kernel, tiles), out_shape=[jax.ShapeDtyp...]
    all_to_all x3 -> x0, blocking collectives: 102 us -> none  [the longest x2 87.3 us: summed_on_arrival(): lax.all_to_all(pieces, axis, split_axis=0, concat_axis=0, tiled=True)]
    dot_general x54 -> x0, matrix products: 65.9 us -> none  [the longest x14 20.8 us: outer_sum(): lax.dot_general(left, right, (((0,), (0,)), ((), ())), preferred_element_...]
    all_to_all x3 -> x0, waiting for transfers between devices: 38.1 us -> none  [copy_for_each(): lax.all_to_all(jnp.broadcast_to(x[None], (peers, *x.shape)), axis, 0, 0,...]
    gather x41 -> x0, local copies, waits for them, and re-layouts: 34.4 us -> none  [the longest x24 20.4 us: block_step(): fetched = jnp.take(sources, picked, axis=0)]
    all_to_all x3 -> x0, starting transfers between devices: 22.9 us -> none  [copy_for_each(): lax.all_to_all(jnp.broadcast_to(x[None], (peers, *x.shape)), axis, 0, 0,...]
    ppermute x6 -> x0, starting transfers between devices: 21.6 us -> none  [the longest x2 12.2 us: with_halo(): lax.ppermute(last, axis, up)]
  transfers between devices with their start and end apart: 10 -> 0, of which waited for: 8 -> 0; matrix products, arithmetic and copies ran while one was open for 1% -> 0% of each run, Pallas kernels for 0% -> 0%
where the time goes in v1:
time: 116 us; the launch traced here: 115 us
  Pallas kernels  109 us (94%)
  other arithmetic  5.5 us (5%)
    pallas_call x1, Pallas kernels, shards(): pl.pallas_call(functools.partial(kernel, tiles), out_shape=[jax.ShapeDtyp...  109 us
    convert_element_type x4, other arithmetic, shards(): return (grid_update, *(g.astype(F32) for g in (eg, dg, mg, sg)))  5.5 us

profile of v1, /device:TPU:1, one launch (start us, length us, event | category | flops | bytes accessed | tf_op | source)
XLA Modules:
  0.0 115.5 jit_solution(1045364935866224019)
XLA Ops:
  0.6 108.7 %shard_map.182 = (bf16[128,512]{1,0:T(8,128)(2,1)}, bf16[512,512]{1,0:T(8,128)(2,1)}, bf16[512,512]{1,0:T(8,128)(2,1)}, bf16[512,512]{1,0:T(8,128)(2,1)}, bf16[512,512]{1,0:T(8,128)(2,1)}) custom-call(bf16[128,512]{1,0:T(8,128)(2,1)} %grid_hbm.1, bf16[128,512]{1,0:T(8,128)(2,1)} %mesh_hbm.1, bf16[1024,512]{1,0:T(8,128)(2,1)} %ee_hbm.1, ...), custom_call_target="tpu_custom_call" | custom-call | tf_op jit(solution)/shard_map/pallas_call | solution.py:617
  109.3 0.0 copy-start.2
  109.3 2.2 %convert_element_type.12 = f32[512,512]{1,0:T(8,128)} convert(bf16[512,512]{1,0:T(8,128)(2,1)} %get-tuple-element.11) | non-fusion elementwise | flops 262144 | bytes 1572864 | tf_op jit(solution)/shard_map/convert_element_type | solution.py:639
  111.5 0.0 copy-done.2
  111.5 0.0 copy-start.1
  111.5 1.1 convert_element_type.13
  112.6 0.0 copy-done.1
  112.6 0.0 copy-start
  112.6 1.1 convert_element_type.14
  113.7 0.0 copy-done
  113.7 0.0 copy-start.3
  113.7 1.1 convert_element_type.15
  114.8 0.0 copy-done.3
  114.8 0.7 copy.21
Async XLA Ops:
  109.3 2.2 %copy-start.2 = (bf16[512,512]{1,0:T(8,128)(2,1)S(1)}, bf16[512,512]{1,0:T(8,128)(2,1)}, u32[]{:S(2)}) copy-start(bf16[512,512]{1,0:T(8,128)(2,1)} %get-tuple-element.12) | copy-start | bytes 1572868
  111.5 1.1 copy-start.1
  112.6 1.1 copy-start
  113.7 1.1 copy-start.3

commit v2 on v1

--- a/solution.py
+++ b/solution.py
@@ -10,8 +10,10 @@
 MESH = pl.DeviceIdType.MESH
 TOP = 512
 LANES = 128
+PARTS = 2
 LAYOUT = {64: (8, 2, 4), 4: (2, 1, 2)}
 F32 = jnp.float32
+VMEM_BYTES = 67043328
 BF16 = jnp.bfloat16
 
 
@@ -78,6 +80,9 @@
     def across(self):
         return (self.tile, lax.rem(self.sub + 2, 4))
 
+    def diagonal(self):
+        return (self.tile, 3 - self.sub)
+
     def beside(self, by):
         d = lax.rem(self.device + by + 4 * self.tiles, 4 * self.tiles)
         return (lax.div(d, 4), lax.rem(d, 4))
@@ -102,95 +107,137 @@
     )
 
 
+def hops(k, n):
+    return min(k, n - k)
+
+
 class Total:
-    def __init__(self, spot, slot, bufs):
-        self.spot, self.slot = spot, slot
-        own, pair, half, planes, column, full, self.ps, self.pr, self.qs, self.qr, self.zs, self.zr = bufs
-        self.own, self.pair, self.half = own.at[slot], pair.at[slot], half.at[slot]
-        self.planes, self.column, self.full = planes.at[slot], column.at[slot], full.at[slot]
-        self.rows = TOP // 2
-        self.block = self.rows // spot.plane
-
-    def half_of(self, core):
-        return pl.ds(pl.multiple_of(core * self.rows, self.rows), self.rows)
-
-    def my_rows(self):
-        s = self.spot
-        start = s.core * self.rows + s.p * self.block
-        return pl.ds(pl.multiple_of(start, self.block), self.block)
+    def __init__(self, spot, slot, part, lead, bufs):
+        self.spot = spot
+        own, pair, half, planes, column, full, ps, pr, qs, qr, zs, zr = bufs
+        width = own.shape[2] // PARTS
+        i = slot * PARTS + part
+        self.cols = pl.ds(part * width, width)
+        self.own, self.full = own.at[slot], full.at[slot]
+        self.pair, self.half, self.planes, self.column = pair.at[i], half.at[i], planes.at[i], column.at[i]
+        self.ps, self.pr, self.qs, self.qr, self.zs, self.zr = (a.at[i] for a in (ps, pr, qs, qr, zs, zr))
+        self.block = TOP // spot.plane
+        self.leads, self.follows = spot.core == lead, spot.core != lead
+        self.peers = sorted(
+            range(1, spot.plane),
+            key=lambda k: -hops(k // spot.nx, spot.ny) - hops(k % spot.nx, spot.nx),
+        )
+        self.rungs = sorted(range(1, spot.nz), key=lambda j: -hops(j, spot.nz))
+
+    def rows_of(self, p):
+        return pl.ds(pl.multiple_of(p * self.block, self.block), self.block)
 
     def pair_copy(self, n):
-        s = self.spot
         if n == 0:
-            src, dst = self.own.at[self.half_of(1 - s.core)], self.pair
+            src, dst = self.own.at[:, self.cols], self.pair
         else:
-            src = dst = self.full.at[self.half_of(s.core)]
-        return remote(src, dst, self.ps.at[self.slot, n], self.pr.at[self.slot, n], s.partner())
+            src = dst = self.full.at[:, self.cols]
+        return remote(src, dst, self.ps, self.pr, self.spot.partner())
 
     def plane_copy(self, n, k):
         q, where = self.spot.in_plane(k)
         if n == 0:
-            src = self.half.at[pl.ds(pl.multiple_of(q * self.block, self.block), self.block)]
-            dst = self.planes.at[k]
+            src, dst = self.half.at[self.rows_of(q)], self.planes.at[k]
         else:
-            src = dst = self.full.at[self.my_rows()]
-        return remote(src, dst, self.qs.at[self.slot, n, k], self.qr.at[self.slot, n, k], where)
+            src = dst = self.full.at[self.rows_of(self.spot.p), self.cols]
+        return remote(src, dst, self.qs, self.qr.at[n], where)
 
     def column_copy(self, j):
-        s = self.spot
-        src = self.column.at[s.z]
-        return remote(src, src, self.zs.at[self.slot, j], self.zr.at[self.slot, j], s.in_column(j))
+        src = self.column.at[self.spot.z]
+        return remote(src, src, self.zs, self.zr, self.spot.in_column(j))
+
+    def plane_done(self, n):
+        all_of = self.planes.at[pl.ds(1, self.spot.plane - 1)]
+        return remote(all_of, all_of, self.qs, self.qr.at[n], self.spot.partner())
+
+    def column_done(self):
+        all_of = self.column.at[pl.ds(1, self.spot.nz - 1)]
+        return remote(all_of, all_of, self.zs, self.zr, self.spot.partner())
 
     def step0(self):
-        self.pair_copy(0).start()
+        @pl.when(self.follows)
+        def _():
+            self.pair_copy(0).start()
 
     def step1(self):
-        self.pair_copy(0).wait_recv()
-        mine = self.own[self.half_of(self.spot.core), :].astype(F32)
-        self.half[...] = (mine + self.pair[...].astype(F32)).astype(BF16)
-        for k in range(1, self.spot.plane):
-            self.plane_copy(0, k).start()
+        @pl.when(self.leads)
+        def _():
+            self.pair_copy(0).wait_recv()
+            mine = self.own[:, self.cols].astype(F32)
+            self.half[...] = (mine + self.pair[...].astype(F32)).astype(BF16)
+            for k in self.peers:
+                self.plane_copy(0, k).start()
 
     def step2(self):
-        s = self.spot
-        start = pl.multiple_of(s.p * self.block, self.block)
-        total = self.half[pl.ds(start, self.block), :].astype(F32)
-        for k in range(1, s.plane):
-            self.plane_copy(0, k).wait_recv()
-        for k in range(1, s.plane):
-            total = total + self.planes[k].astype(F32)
-        self.column[s.z] = total.astype(BF16)
-        for j in range(1, s.nz):
-            self.column_copy(j).start()
+        @pl.when(self.leads)
+        def _():
+            total = self.half[self.rows_of(self.spot.p), :].astype(F32)
+            self.plane_done(0).wait_recv()
+            for k in self.peers:
+                total = total + self.planes[k].astype(F32)
+            self.column[self.spot.z] = total.astype(BF16)
+            for j in self.rungs:
+                self.column_copy(j).start()
 
     def step3(self, scale=None):
-        s = self.spot
-        for j in range(1, s.nz):
-            self.column_copy(j).wait_recv()
-        total = self.column[0].astype(F32)
-        for j in range(1, s.nz):
-            total = total + self.column[j].astype(F32)
-        if scale is not None:
-            total = total * scale
-        self.full[self.my_rows(), :] = total.astype(BF16)
-        for k in range(1, s.plane):
-            self.plane_copy(1, k).start()
+        @pl.when(self.leads)
+        def _():
+            self.column_done().wait_recv()
+            self.plane_done(0).wait_send()
+            total = self.column[0].astype(F32)
+            for j in range(1, self.spot.nz):
+                total = total + self.column[j].astype(F32)
+            if scale is not None:
+                total = total * scale
+            self.full[self.rows_of(self.spot.p), self.cols] = total.astype(BF16)
+            for k in self.peers:
+                self.plane_copy(1, k).start()
 
     def step4(self):
-        for k in range(1, self.spot.plane):
-            self.plane_copy(1, k).wait_recv()
-        self.pair_copy(1).start()
+        @pl.when(self.leads)
+        def _():
+            self.plane_done(1).wait_recv()
+            self.pair_copy(1).start()
 
     def step5(self):
-        self.pair_copy(1).wait_recv()
+        @pl.when(self.follows)
+        def _():
+            self.pair_copy(1).wait_recv()
 
     def drain(self):
-        for n in range(2):
-            self.pair_copy(n).wait_send()
-            for k in range(1, self.spot.plane):
-                self.plane_copy(n, k).wait_send()
-        for j in range(1, self.spot.nz):
-            self.column_copy(j).wait_send()
+        @pl.when(self.follows)
+        def _():
+            self.pair_copy(0).wait_send()
+
+        @pl.when(self.leads)
+        def _():
+            self.pair_copy(1).wait_send()
+            self.plane_done(1).wait_send()
+            self.column_done().wait_send()
+
+
+class Parts:
+    def __init__(self, spot, slot, lead, bufs):
+        self.own, self.full = bufs[0].at[slot], bufs[5].at[slot]
+        self.parts = [Total(spot, slot, i, lead, bufs) for i in range(PARTS)]
+
+    def fill(self, part_of):
+        for part in self.parts:
+            self.own[:, part.cols] = part_of(part.cols).astype(BF16)
+            part.step0()
+
+    def step(self, n, *given):
+        for part in self.parts:
+            getattr(part, f"step{n}")(*given)
+
+    def drain(self):
+        for part in self.parts:
+            part.drain()
 
 
 def kernel(
@@ -199,12 +246,12 @@
     mesh_hbm,
     ee_hbm,
     de_hbm,
-    esrc,
-    etgt,
-    dsrc,
-    dtgt,
-    fine,
-    coarse,
+    esrc_hbm,
+    etgt_hbm,
+    dsrc_hbm,
+    dtgt_hbm,
+    fine_hbm,
+    coarse_hbm,
     we_hbm,
     wd_hbm,
     wm_hbm,
@@ -215,6 +262,12 @@
     out_d,
     out_m,
     out_s,
+    esrc,
+    etgt,
+    dsrc,
+    dtgt,
+    fine,
+    coarse,
     gw,
     mesh,
     ee,
@@ -242,7 +295,6 @@
     sile,
     ssle,
     sild,
-    ssld,
     mid,
     sub_src,
     sub_dst,
@@ -262,6 +314,10 @@
     up,
     sslope,
     sback,
+    ce,
+    own_slope,
+    gout,
+    sgrad,
     own,
     pair,
     half,
@@ -269,6 +325,7 @@
     column,
     full,
     lsem,
+    osem,
     hs,
     hr,
     ss,
@@ -287,7 +344,9 @@
     enc_factor, dec_factor = n / n_enc, n / n_dec
     mid_factor, top_factor = 0.25, TOP / (n * tiles)
     bufs = (own, pair, half, planes, column, full, ps, pr, qs, qr, zs, zr)
-    t_sum, t_back, t_dec, t_mid, t_enc = (Total(spot, i, bufs) for i in range(5))
+    t_sum, t_back, t_dec, t_mid, t_enc = (
+        Parts(spot, i, lead, bufs) for i, lead in enumerate((1, 1, 0, 0, 1))
+    )
 
     loads = [
         pltpu.make_async_copy(src, dst, lsem.at[i])
@@ -302,14 +361,20 @@
                 (wd_hbm, wd),
                 (de_hbm, de),
                 (cot_hbm, cot),
+                (fine_hbm, fine),
+                (coarse_hbm, coarse),
+                (esrc_hbm, esrc),
+                (etgt_hbm, etgt),
+                (dsrc_hbm, dsrc),
+                (dtgt_hbm, dtgt),
             )
         )
     ]
-    for copy in loads:
+    for copy in loads[9:] + loads[:9]:
         copy.start()
 
     barrier = pltpu.get_barrier_semaphore()
-    greeted = [spot.beside(1), spot.beside(-1), spot.partner(), spot.across()]
+    greeted = [spot.beside(1), spot.beside(-1), spot.partner(), spot.across(), spot.diagonal()]
     greeted += [spot.in_plane(k)[1] for k in range(1, spot.plane)]
     greeted += [spot.in_column(j) for j in range(1, spot.nz)]
     for where in greeted:
@@ -328,6 +393,8 @@
             by_edge[i * n : (i + 1) * n, j * n : (j + 1) * n] = ones_where(down == lane + j * n)
             by_node[j * n : (j + 1) * n, i * n : (i + 1) * n] = ones_where(across == row + j * n)
 
+    for copy in loads[9:]:
+        copy.wait()
     first = spot.device * n
     across, down = spread(fine, 0, spot.tile * n)
     fm[...] = ones_where(across == row)
@@ -381,30 +448,36 @@
 
     def sub_copy(i):
         where = spot.partner() if i % 2 == 0 else spot.across()
-        return remote(sub_src.at[i], sub_dst.at[i], ss.at[i], sr.at[i], where)
+        src, dst = sub_src.at[i], sub_dst.at[i]
+        if i == 1:
+            theirs = quarter(lax.rem(spot.sub + 2, 4))
+            src, dst = src.at[theirs], dst.at[theirs]
+        return remote(src, dst, ss.at[i], sr.at[i], where)
+
+    def quarter(sub):
+        return pl.ds(pl.multiple_of(sub * (n // 4), n // 4), n // 4)
+
+    def quarter_copies():
+        part = midin.at[quarter(spot.sub)]
+        peers = (spot.partner(), spot.across(), spot.diagonal())
+        return [remote(part, part, ss.at[4 + i], sr.at[4 + i], where) for i, where in enumerate(peers)]
 
     sub_src[0] = nn(fm[...], mid_value).astype(BF16)
     sub_copy(0).start()
+    midout[...] = jnp.zeros_like(midout)
     sub_copy(0).wait_recv()
     sub_src[1] = (sub_src[0].astype(F32) + sub_dst[0].astype(F32)).astype(BF16)
     sub_copy(1).start()
     loads[4].wait()
     sub_copy(1).wait_recv()
-    middle_in = (mid_factor * (sub_src[1].astype(F32) + sub_dst[1].astype(F32))).astype(BF16)
-    midin[...] = middle_in
-    act, sloped = silu_pair(nn(middle_in, wm[...]))
-    midss[...] = sloped
-    middle_out = (middle_in.astype(F32) + act).astype(BF16)
-    wide_row = lax.broadcasted_iota(jnp.int32, (n, d), 0)
-    mine = (wide_row >= spot.sub * (n // 4)) & (wide_row < (spot.sub + 1) * (n // 4))
-    midout[...] = jnp.where(mine, middle_out.astype(F32), 0.0).astype(BF16)
-    t_sum.own[...] = nn(kc[...], midout[...]).astype(BF16)
-    t_sum.step0()
-    base[middle, :] = mid[...].astype(F32) + nn(ft[...], middle_out)
-    t_sum.step1()
-    base_halo = both_ways(base, 4, low, middle, high)
-    for copy in base_halo:
+    at = quarter(spot.sub)
+    part_in = (mid_factor * (sub_src[1, at, :].astype(F32) + sub_dst[1, at, :].astype(F32))).astype(BF16)
+    midin[at, :] = part_in
+    midout[at, :] = (part_in.astype(F32) + silu_pair(nn(part_in, wm[...]))[0]).astype(BF16)
+    t_sum.fill(lambda cols: nn(kc[...], midout[:, cols]))
+    for copy in quarter_copies():
         copy.start()
+    t_sum.step(1)
     for copy in ids_halo:
         copy.wait_recv()
     for i in range(3):
@@ -413,14 +486,30 @@
         for j in range(TOP // n):
             cw[j * n : (j + 1) * n, i * n : (i + 1) * n] = ones_where(around == row + j * n)
             cwt[i * n : (i + 1) * n, j * n : (j + 1) * n] = ones_where(along == lane + j * n)
-    t_sum.step2()
-    t_sum.step3(top_factor)
+    for copy in quarter_copies():
+        copy.wait_recv()
+    act, sloped = silu_pair(nn(midin[...], wm[...]))
+    midss[...] = sloped
+    middle_out = (midin[...].astype(F32) + act).astype(BF16)
+    base[middle, :] = mid[...].astype(F32) + nn(ft[...], middle_out)
+    base_halo = both_ways(base, 4, low, middle, high)
+
+    def edge_tops(at):
+        ce[at, :] = nn(cw[at, :], std[...]).astype(BF16)
+
+    chunks(TOP // 256, 256, edge_tops)
+    wide_row = lax.broadcasted_iota(jnp.int32, (n, d), 0)
+    mine = (wide_row >= spot.sub * (n // 4)) & (wide_row < (spot.sub + 1) * (n // 4))
+    t_sum.step(2)
+    for copy in base_halo:
+        copy.start()
+    t_sum.step(3, top_factor)
     for i in range(5, 9):
         loads[i].wait()
     for copy in base_halo:
         copy.wait_recv()
-    t_sum.step4()
-    t_sum.step5()
+    t_sum.step(4)
+    t_sum.step(5)
 
     def top(at):
         act, sloped = silu_pair(nn(t_sum.full[at, :], ws[...]))
@@ -443,48 +532,56 @@
 
     chunks(n_dec // 256, 256, decode)
 
+    def top_edges(at):
+        sslope[at, :] = nn(ce[at, :], slope[pl.ds(0, n_dec), :]).astype(BF16)
+
+    chunks(TOP // 256, 256, top_edges)
+    t_back.fill(lambda cols: nt(sslope[...], wd[cols, :]))
+    t_back.step(1)
     def back(at):
         spread_slope = nn(std[at, :], slope[pl.ds(0, n_dec), :]).astype(BF16)
         tw[at, :] = spread_slope
         rw[at, :] = nt(spread_slope, wd[...]).astype(BF16)
 
     chunks(3, n, back)
-
-    def top_part(at):
-        t_back.own[at, :] = nn(cw[at, :], rw[...]).astype(BF16)
-
-    chunks(TOP // 256, 256, top_part)
-    t_back.step0()
     back_halo = (
         beside_copy(rw.at[high], rback.at[0], 6, 1),
         beside_copy(rw.at[low], rback.at[1], 7, -1),
     )
-    t_back.step1()
     for copy in back_halo:
         copy.start()
-    t_dec.own[...] = tn(mow[...], tw[...]).astype(BF16)
-    t_dec.step0()
-    out_grid[...] = (
-        gw[middle, :].astype(F32) + dec_factor * nn(md[...], sild[...])
-    ).astype(BF16)
+    t_dec.fill(lambda cols: tn(mow[...], tw[:, cols]))
+    gout[...] = (gw[middle, :].astype(F32) + dec_factor * nn(md[...], sild[...])).astype(BF16)
+    put = [
+        pltpu.make_async_copy(src, dst, osem.at[i])
+        for i, (src, dst) in enumerate(
+            (
+                (gout, out_grid),
+                (sgrad, out_s),
+                (t_dec.full, out_d),
+                (t_mid.full, out_m),
+                (t_enc.full, out_e),
+            )
+        )
+    ]
+    put[0].start()
+    t_back.step(2)
+    t_dec.step(1)
     for copy in back_halo:
         copy.wait_recv()
     mesh_grad = rw[middle, :].astype(F32) + rback[0].astype(F32) + rback[1].astype(F32)
     meshg[...] = mesh_grad
     sub_src[2] = sum_halves(fm[...], mesh_grad).astype(BF16)
     sub_copy(2).start()
-    t_back.step2()
-    t_dec.step1()
     sub_copy(2).wait_recv()
     sub_src[3] = (sub_src[2].astype(F32) + sub_dst[2].astype(F32)).astype(BF16)
     sub_copy(3).start()
-    t_back.step3()
-    t_dec.step2()
+    t_back.step(3)
+    t_dec.step(2)
     sub_copy(3).wait_recv()
     lev[...] = sub_src[3].astype(F32) + sub_dst[3].astype(F32)
-    t_back.step4()
-    t_back.step5()
-
+    t_back.step(4)
+    t_back.step(5)
     def top_slope(at):
         value = (t_back.full[at, :].astype(F32) * sumss[at, :]).astype(BF16)
         sslope[at, :] = value
@@ -493,13 +590,12 @@
     chunks(TOP // 256, 256, top_slope)
     level_total = lev[...] + top_factor * nn(kt[...], sback[...])
     middle_slope = (level_total * midss[...]).astype(BF16)
-    own_slope = jnp.where(mine, middle_slope.astype(F32), 0.0).astype(BF16)
-    t_mid.own[...] = tn(midin[...], own_slope).astype(BF16)
-    t_mid.step0()
+    own_slope[...] = jnp.where(mine, middle_slope.astype(F32), 0.0).astype(BF16)
+    t_mid.fill(lambda cols: tn(midin[...], own_slope[:, cols]))
     middle_back = level_total + nt(middle_slope, wm[...])
     mesh_total = meshg[...] + mid_factor * nn(ft[...], middle_back.astype(BF16))
     up[...] = mesh_total.astype(BF16)
-
+    t_dec.step(3)
     def encode_back(at):
         upstream = nn(mte[at, :], up[...]) * enc_factor
         slope[at, :] = (upstream * ssle[at, :]).astype(BF16)
@@ -510,28 +606,50 @@
         tw[at, :] = nn(ste[at, :], slope[...]).astype(BF16)
 
     chunks(3, n, encode_spread)
-    t_enc.own[...] = tn(gw[...], tw[...]).astype(BF16)
-    t_enc.step0()
-    t_mid.step1()
-    t_enc.step1()
-    t_dec.step3()
-    t_mid.step2()
-    t_enc.step2()
-    out_s[...] = tn(t_sum.full[...], sslope[...]).astype(BF16)
-    t_mid.step3()
-    t_enc.step3()
-    t_dec.step4()
-    t_mid.step4()
-    t_enc.step4()
-    for total, out in ((t_dec, out_d), (t_mid, out_m), (t_enc, out_e)):
-        total.step5()
-        out[...] = total.full[...]
+    t_enc.fill(lambda cols: tn(gw[...], tw[:, cols]))
+    t_mid.step(1)
+    t_enc.step(1)
+    sgrad[...] = tn(t_sum.full[...], sslope[...]).astype(BF16)
+    put[1].start()
+    t_dec.step(4)
+    t_mid.step(2)
+    t_enc.step(2)
+    t_dec.step(5)
+    put[2].start()
+    t_mid.step(3)
+    t_enc.step(3)
+    t_mid.step(4)
+    t_enc.step(4)
+    t_mid.step(5)
+    put[3].start()
+    t_enc.step(5)
+    put[4].start()
     for total in (t_sum, t_back, t_dec, t_mid, t_enc):
         total.drain()
+    for copy in put:
+        copy.wait()
     for copy in grid_halo + ids_halo + base_halo + back_halo:
         copy.wait_send()
-    for i in range(4):
-        sub_copy(i).wait_send()
+    for copy in [sub_copy(i) for i in range(4)] + quarter_copies():
+        copy.wait_send()
+
+
+def widen(*refs):
+    given, out = refs[:5], refs[5:10]
+    rows, narrow, wide, in_sem, out_sem = refs[10:]
+    sources = [rows] + [narrow.at[i] for i in range(4)]
+    results = [rows] + [wide.at[i] for i in range(4)]
+    taken = [pltpu.make_async_copy(a, b, in_sem.at[i]) for i, (a, b) in enumerate(zip(given, sources))]
+    put = [pltpu.make_async_copy(a, b, out_sem.at[i]) for i, (a, b) in enumerate(zip(results, out))]
+    for copy in taken:
+        copy.start()
+    for i in range(5):
+        taken[i].wait()
+        if i:
+            results[i][...] = sources[i][...].astype(F32)
+        put[i].start()
+    for copy in put:
+        copy.wait()
 
 
 def shards(tiles, *args):
@@ -541,14 +659,14 @@
     nz, nyh, nx = LAYOUT[tiles]
     plane = 2 * nyh * nx
     hbm = pl.BlockSpec(memory_space=pl.ANY)
-    vmem = pl.BlockSpec(memory_space=pltpu.VMEM)
 
     def v(*shape, dtype=BF16):
         return pltpu.VMEM(shape, dtype)
 
     sem = lambda *shape: pltpu.SemaphoreType.DMA(shape)
-    wide = 3 * n
+    wide, streams = 3 * n, 5 * PARTS
     scratch = [
+        *(v(r // LANES, LANES, dtype=jnp.int32) for r in (ne, ne, nd, nd, n, n)),
         v(wide, d),
         v(n, d),
         v(ne, d),
@@ -576,7 +694,6 @@
         v(ne, d),
         v(ne, d, dtype=F32),
         v(nd, d),
-        v(nd, d, dtype=F32),
         v(n, d),
         v(4, n, d),
         v(4, n, d),
@@ -596,33 +713,38 @@
         v(n, d),
         v(TOP, d),
         v(TOP, d),
+        v(TOP, nd),
+        v(n, d),
+        v(n, d),
+        v(d, d),
         v(5, TOP, d),
-        v(5, TOP // 2, d),
-        v(5, TOP // 2, d),
-        v(5, plane, TOP // 2 // plane, d),
-        v(5, nz, TOP // 2 // plane, d),
+        v(streams, TOP, d // PARTS),
+        v(streams, TOP, d // PARTS),
+        v(streams, plane, TOP // plane, d // PARTS),
+        v(streams, nz, TOP // plane, d // PARTS),
         v(5, TOP, d),
-        sem(9),
+        sem(15),
+        sem(5),
         sem(8),
         sem(8),
-        sem(4),
-        sem(4),
-        sem(5, 2),
-        sem(5, 2),
-        sem(5, 2, plane),
-        sem(5, 2, plane),
-        sem(5, nz),
-        sem(5, nz),
+        sem(7),
+        sem(7),
+        sem(streams),
+        sem(streams),
+        sem(streams),
+        sem(streams, 2),
+        sem(streams),
+        sem(streams),
     ]
-    grid_update, eg, dg, mg, sg = pl.pallas_call(
+    results = pl.pallas_call(
         functools.partial(kernel, tiles),
         out_shape=[jax.ShapeDtypeStruct((n, d), BF16)]
         + [jax.ShapeDtypeStruct((d, d), BF16)] * 4,
-        in_specs=[hbm] * 4 + [vmem] * 6 + [hbm] * 5,
-        out_specs=[vmem] * 5,
+        in_specs=[hbm] * 15,
+        out_specs=[hbm] * 5,
         scratch_shapes=scratch,
         compiler_params=pltpu.CompilerParams(
-            collective_id=0, has_side_effects=True, vmem_limit_bytes=60 * 1024 * 1024
+            collective_id=0, has_side_effects=True, vmem_limit_bytes=VMEM_BYTES
         ),
     )(
         gf,
@@ -636,7 +758,15 @@
         ws,
         cot,
     )
-    return (grid_update, *(g.astype(F32) for g in (eg, dg, mg, sg)))
+    return pl.pallas_call(
+        widen,
+        out_shape=[jax.ShapeDtypeStruct((n, d), BF16)]
+        + [jax.ShapeDtypeStruct((d, d), F32)] * 4,
+        in_specs=[hbm] * 5,
+        out_specs=[hbm] * 5,
+        scratch_shapes=[v(n, d), v(4, d, d), v(4, d, d, dtype=F32), sem(5), sem(5)],
+        compiler_params=pltpu.CompilerParams(vmem_limit_bytes=VMEM_BYTES),
+    )(*results)
 
 
 def solution(mesh):

time: 116 us -> 102 us (0.88)
  Pallas kernels: 109 us -> 101 us
  other arithmetic: 5.5 us -> 0 us
    pallas_call x1, Pallas kernels: 109 us -> 98.1 us  [shards(): pl.pallas_call(functools.partial(kernel, tiles), out_shape=[jax.ShapeDtyp...]
    convert_element_type x4 -> x0, other arithmetic: 5.5 us -> none  [shards(): return (grid_update, *(g.astype(F32) for g in (eg, dg, mg, sg)))]
    pallas_call x0 -> x1, Pallas kernels: none -> 3.28 us  [shards(): pl.pallas_call(widen, out_shape=[jax.ShapeDtypeStruct((n, d), BF16)] + [j...]
where the time goes in v2:
time: 102 us
  Pallas kernels  101 us (99%)
    pallas_call x1, Pallas kernels, shards(): pl.pallas_call(functools.partial(kernel, tiles), out_shape=[jax.ShapeDtyp...  98.1 us
    pallas_call x1, Pallas kernels, shards(): pl.pallas_call(widen, out_shape=[jax.ShapeDtypeStruct((n, d), BF16)] + [j...  3.28 us

profile of v2, /device:TPU:1, one launch (start us, length us, event | category | flops | bytes accessed | tf_op | source)
XLA Modules:
  0.0 102.1 jit_solution(2271532573315478124)
XLA Ops:
  0.6 98.1 %shard_map.182 = (bf16[128,512]{1,0:T(8,128)(2,1)}, bf16[512,512]{1,0:T(8,128)(2,1)}, bf16[512,512]{1,0:T(8,128)(2,1)}, bf16[512,512]{1,0:T(8,128)(2,1)}, bf16[512,512]{1,0:T(8,128)(2,1)}) custom-call(bf16[128,512]{1,0:T(8,128)(2,1)} %grid_hbm.1, bf16[128,512]{1,0:T(8,128)(2,1)} %mesh_hbm.1, bf16[1024,512]{1,0:T(8,128)(2,1)} %ee_hbm.1, ...), custom_call_target="tpu_custom_call" | custom-call | tf_op jit(solution)/shard_map/pallas_call | solution.py:739
  98.8 3.3 %shard_map.183 = (bf16[128,512]{1,0:T(8,128)(2,1)}, f32[512,512]{1,0:T(8,128)}, f32[512,512]{1,0:T(8,128)}, f32[512,512]{1,0:T(8,128)}, f32[512,512]{1,0:T(8,128)}) custom-call(bf16[128,512]{1,0:T(8,128)(2,1)} %get-tuple-element.10.refs_0_, bf16[512,512]{1,0:T(8,128)(2,1)} %get-tuple-element.11.refs_1_, bf16[512,512]{1,0:T(8,128)(2,1)} %get-tuple-element.12.refs_2_, ...), custom_call_target="tpu_custom_call" | custom-call | tf_op jit(solution)/shard_map/pallas_call | solution.py:761
